TPU v7x, 256 devices: a whole 4x4x8 slice. The times are simulated.
256 devices in a mesh: dp: 8 (over y, core), expert: 32 (over x, z).
Axes of the slice: x: 4, y: 4, z: 8, core: 2. Of those that a mesh axis runs over, the one named last changes fastest.
Arguments:
- tokens: bfloat16 [32768, 2048], P(('dp', 'expert')), may hold values from -6 to 6
- out_grad: bfloat16 [32768, 2048], P(('dp', 'expert')), may hold values from -3 to 3
- expert_ids: int32 [32768, 8], P(('dp', 'expert')), may hold values from 0 to 63, all different within a row; in each aligned block of 128 rows (0 to 127, 128 to 255, ...) at most 17 rows name the same one
- gate_probs: bfloat16 [32768, 8], P(('dp', 'expert')), may hold values from 0.019897461 to 0.3984375
- gate_up_weight: bfloat16 [64, 2048, 768], P('expert'), may hold values from -0.125 to 0.125
- down_weight: bfloat16 [64, 384, 2048], P('expert'), may hold values from -0.3125 to 0.3125
Outputs:
- grad_tokens: bfloat16 [32768, 2048], P(('dp', 'expert'))
- grad_probs: bfloat16 [32768, 8], P(('dp', 'expert'))
- grad_weights: bfloat16 [2048, 64, 1152], P('dp', 'expert')
Inputs may be any that keep to these rules, and one draw needn't show every extreme that they name: `expert_ids`: each row names 8 distinct experts; in each aligned block of 128 rows no expert is named by more than 17 rows.
All inputs are finite; a program needn't handle non-finite values.
Results may differ from a plain program's by a relative error of at most 0.013.
Values may be sent and summed in bfloat16 or wider, within the bound.
A program may use at most 128 MiB of HBM per device.

v0:
```python
import jax
import jax.numpy as jnp
from jax import lax
from jax.sharding import PartitionSpec as P


def silu_parts(gate_pre):
    logistic = jax.nn.sigmoid(gate_pre)
    return (gate_pre * logistic, logistic * (1.0 + gate_pre * (1.0 - logistic)))


def on_device(tokens, out_grad, expert_ids, gate_probs, gate_up_weight, down_weight):
    token_rows, model_width = tokens.shape
    top_count = expert_ids.shape[1]
    local_experts = gate_up_weight.shape[0]
    hidden_units = down_weight.shape[1]
    peer_count = lax.axis_size("expert")
    expert_count = local_experts * peer_count
    pair_count = token_rows * top_count
    capacity = pair_count // expert_count + max(1, pair_count // (16 * expert_count))
    row_count = peer_count * capacity
    slot_count = local_experts * row_count
    flat_ids = expert_ids.reshape(-1)
    onehot = (flat_ids[:, None] == jnp.arange(expert_count, dtype=jnp.int32)[None, :]).astype(
        jnp.int32
    )
    ranking = jnp.sum((jnp.cumsum(onehot, axis=0) - onehot) * onehot, axis=1)
    placement = (
        flat_ids % local_experts * peer_count + flat_ids // local_experts
    ) * capacity + ranking
    source = (
        jnp.full((slot_count,), pair_count, jnp.int32)
        .at[placement]
        .set(jnp.arange(pair_count, dtype=jnp.int32))
    )
    filled = source < pair_count
    clipped = jnp.minimum(source, pair_count - 1)
    owner_token = clipped // top_count
    block_shape = (local_experts, peer_count, capacity, model_width)
    send_inputs = jnp.where(filled[:, None], tokens[owner_token], 0).reshape(block_shape)
    send_cotangent = jnp.where(filled[:, None], out_grad[owner_token], 0).reshape(block_shape)
    send_weights = jnp.where(filled, gate_probs.reshape(-1)[clipped], 0).reshape(
        local_experts, peer_count, capacity
    )
    recv_inputs, recv_cotangent, recv_weights = (
        lax.all_to_all(send_inputs, "expert", split_axis=1, concat_axis=1, tiled=True),
        lax.all_to_all(send_cotangent, "expert", split_axis=1, concat_axis=1, tiled=True),
        lax.all_to_all(send_weights, "expert", split_axis=1, concat_axis=1, tiled=True),
    )
    forward_inputs_rows = recv_inputs.reshape(local_experts, row_count, model_width)
    pre_acts = jnp.einsum(
        "erd,edf->erf", forward_inputs_rows, gate_up_weight, preferred_element_type=jnp.float32
    )
    gate_pre = pre_acts[:, :, :hidden_units]
    up_pre = pre_acts[:, :, hidden_units:]
    active, slope_terms = silu_parts(gate_pre)
    forward_hidden = (active * up_pre).astype(jnp.bfloat16)
    expert_out = jnp.einsum(
        "erf,efd->erd", forward_hidden, down_weight, preferred_element_type=jnp.float32
    )
    inputs_rows, up_pre, active, slope_terms, hidden, expert_out = (
        forward_inputs_rows,
        up_pre,
        active,
        slope_terms,
        forward_hidden,
        expert_out,
    )
    cotangent = recv_cotangent.reshape(local_experts, row_count, model_width).astype(jnp.float32)
    weights_rows = recv_weights.reshape(local_experts, row_count).astype(jnp.float32)
    gate_grad = jnp.sum(cotangent * expert_out, axis=2).astype(jnp.bfloat16)
    scaled = (weights_rows[:, :, None] * cotangent).astype(jnp.bfloat16)
    grad_hidden = jnp.einsum(
        "erd,efd->erf", scaled, down_weight, preferred_element_type=jnp.float32
    )
    grad_pre = jnp.concatenate(
        [grad_hidden * up_pre * slope_terms, grad_hidden * active], axis=2
    ).astype(jnp.bfloat16)
    row_grad = jnp.einsum(
        "erf,edf->erd", grad_pre, gate_up_weight, preferred_element_type=jnp.float32
    ).astype(jnp.bfloat16)
    first = jnp.einsum("erd,erf->def", inputs_rows, grad_pre, preferred_element_type=jnp.float32)
    second = jnp.einsum("erd,erf->def", scaled, hidden, preferred_element_type=jnp.float32)
    weight_total = lax.psum_scatter(
        jnp.concatenate([first, second], axis=2).astype(jnp.bfloat16),
        "dp",
        scatter_dimension=0,
        tiled=True,
    )
    back_rows, back_gate = (
        lax.all_to_all(
            row_grad.reshape(block_shape), "expert", split_axis=1, concat_axis=1, tiled=True
        ),
        lax.all_to_all(
            gate_grad.reshape(local_experts, peer_count, capacity),
            "expert",
            split_axis=1,
            concat_axis=1,
            tiled=True,
        ),
    )
    pair_rows = back_rows.reshape(slot_count, model_width)[placement]
    grad_tokens = jnp.sum(
        pair_rows.reshape(token_rows, top_count, model_width).astype(jnp.float32), axis=1
    ).astype(jnp.bfloat16)
    grad_probs = back_gate.reshape(slot_count)[placement].reshape(token_rows, top_count)
    return (grad_tokens, grad_probs, weight_total)


def solution(mesh):
    in_specs = (
        P(("dp", "expert"), None),
        P(("dp", "expert"), None),
        P(("dp", "expert"), None),
        P(("dp", "expert"), None),
        P("expert", None, None),
        P("expert", None, None),
    )
    out_specs = (P(("dp", "expert"), None), P(("dp", "expert"), None), P("dp", "expert", None))
    return jax.shard_map(
        on_device, mesh=mesh, in_specs=in_specs, out_specs=out_specs, check_vma=False
    )
```

profile of v0, /device:TPU:24, one launch (start us, length us, event | category | flops | bytes accessed | tf_op | source)
XLA Modules:
  0.0 582.3 jit_solution(15829125222816076824)
XLA Ops:
  7.2 0.0 copy-start
  7.2 0.9 copy.50
  8.1 0.1 eq.31
  8.2 0.1 eq.27
  8.3 0.1 reshape.198
  8.4 0.8 copy.55
  9.2 0.1 reshape.200
  9.3 0.7 fusion.9
  10.0 31.1 %reduce-window.6 = s32[64,8,128]{2,1,0:T(8,128)S(1)} reduce-window(s32[64,8,128]{2,1,0:T(8,128)} %fusion.9, s32[]{:T(128)} %constant.51.clone.1), window={size=1x1x128 pad=0_0x0_0x127_0}, to_apply=%region_0.0 | reduce-window | flops 8323072 | bytes 524292 | tf_op jit(solution)/shard_map/reduce-window
  41.1 0.8 slice.26
  42.0 1.1 copy.53
  43.1 0.1 copy.54
  43.2 0.1 broadcast_add_fusion
  43.3 0.1 fusion.8
  43.4 4.3 scatter_custom_fusion
  47.8 6.9 %gather_fusion = bf16[1088]{0:T(1024)(128)(2,1)S(1)} fusion(bf16[1024]{0:T(1024)(128)(2,1)S(1)} %reshape.200, s32[2048]{0:T(1024)S(1)} %get-tuple-element.25), kind=kCustom, calls=%fused_computation | custom fusion | bytes 8704 | tf_op jit(solution)/shard_map/gather | solution.py:42
  54.8 0.1 reshape.201
  54.9 0.6 copy.56
  55.5 11.5 %all-to-all-start = ((bf16[2,32,17]{2,0,1:T(2,128)(2,1)}), bf16[2,32,17]{2,0,1:T(2,128)(2,1)S(1)}, u32[]{:S(2)}, u32[]{:S(2)}) async-start(bf16[2,32,17]{2,0,1:T(2,128)(2,1)} %copy.56), calls=%async_computation | async-start | bytes 32768 | tf_op jit(solution)/shard_map/all_to_all | solution.py:48
  67.1 0.1 broadcast_in_dim.38
  67.2 11.7 %gather_fusion.2 = bf16[1088,2048]{1,0:T(8,128)(2,1)} fusion(bf16[128,2048]{1,0:T(8,128)(2,1)} %param.6, s32[2048]{0:T(1024)S(1)} %get-tuple-element.24), kind=kCustom, calls=%fused_computation.2 | custom fusion | bytes 8917248 | tf_op jit(solution)/shard_map/gather | solution.py:40
  78.9 7.6 %gather.23 = bf16[2,32,17,2048]{3,2,1,0:T(8,128)(2,1)} reshape(bf16[1088,2048]{1,0:T(8,128)(2,1)} %gather_fusion.2) | data formatting | bytes 8912896 | tf_op jit(solution)/shard_map/gather | solution.py:40
  86.5 11.7 %gather_fusion.1 = bf16[1088,2048]{1,0:T(8,128)(2,1)} fusion(bf16[128,2048]{1,0:T(8,128)(2,1)} %param.7, s32[2048]{0:T(1024)S(1)} %get-tuple-element.24), kind=kCustom, calls=%fused_computation.1 | custom fusion | bytes 8917248 | tf_op jit(solution)/shard_map/gather | solution.py:41
  98.1 7.6 %gather.21 = bf16[2,32,17,2048]{3,2,1,0:T(8,128)(2,1)} reshape(bf16[1088,2048]{1,0:T(8,128)(2,1)} %gather_fusion.1) | data formatting | bytes 8912896 | tf_op jit(solution)/shard_map/gather | solution.py:41
  105.8 10.3 %broadcast_select_fusion = (bf16[2,32,17,2048]{3,2,1,0:T(8,128)(2,1)}, bf16[2,32,17,2048]{3,2,1,0:T(8,128)(2,1)}) fusion(bf16[2,32,17,2048]{3,2,1,0:T(8,128)(2,1)} %gather.23, pred[2,32,17]{2,1,0:T(8,128)(4,1)S(1)} %broadcast_in_dim.38, bf16[2,32,17,2048]{3,2,1,0:T(8,128)(2,1)} %gather.21), kind=kLoop, calls=%fused_computation.10 | loop fusion | flops 4456448 | bytes 17826880 | tf_op jit(solution)/shard_map/jit(_where)/select_n | solution.py:40
  116.1 9.6 %copy.59 = bf16[2,32,17,2048]{3,0,2,1:T(2,128)(2,1)} copy(bf16[2,32,17,2048]{3,2,1,0:T(8,128)(2,1)} %get-tuple-element.21) | data formatting | bytes 8912896 | tf_op jit(solution)/shard_map/jit(_where)/select_n | solution.py:41
  125.7 0.0 all-to-all-done
  125.7 10.4 %all-to-all-start.1 = ((bf16[2,32,17,2048]{3,0,2,1:T(2,128)(2,1)}), bf16[2,32,17,2048]{3,0,2,1:T(2,128)(2,1)}, u32[]{:S(2)}, u32[]{:S(2)}) async-start(bf16[2,32,17,2048]{3,0,2,1:T(2,128)(2,1)} %copy.59), calls=%async_computation.1 | async-start | bytes 8912896 | tf_op jit(solution)/shard_map/all_to_all | solution.py:47
  136.1 9.7 %copy.61 = bf16[2,32,17,2048]{3,0,2,1:T(2,128)(2,1)} copy(bf16[2,32,17,2048]{3,2,1,0:T(8,128)(2,1)} %get-tuple-element.20) | data formatting | bytes 8912896 | tf_op jit(solution)/shard_map/jit(_where)/select_n | solution.py:40
  145.8 92.4 %all-to-all-done.1 = bf16[2,32,17,2048]{3,0,2,1:T(2,128)(2,1)} async-done(((bf16[2,32,17,2048]{3,0,2,1:T(2,128)(2,1)}), bf16[2,32,17,2048]{3,0,2,1:T(2,128)(2,1)}, u32[]{:S(2)}, u32[]{:S(2)}) %all-to-all-start.1) | async-done | bytes 4456480 | tf_op jit(solution)/shard_map/all_to_all | solution.py:47
  238.2 5.1 all-to-all-start.2
  243.4 0.0 reduce-scatter.2.cloned.1.call-start
  243.4 0.1 copy.57
  243.5 0.1 copy.58
  243.6 0.1 reshape.208
  243.7 11.0 %convert.21 = f32[2,544,2048]{2,0,1:T(2,128)} convert(bf16[2,544,2048]{2,0,1:T(2,128)(2,1)} %bitcast.8) | non-fusion elementwise | flops 2228224 | bytes 13369344 | tf_op jit(solution)/shard_map/convert_element_type | solution.py:69
  254.7 89.8 %all-to-all-done.2 = bf16[2,32,17,2048]{3,0,2,1:T(2,128)(2,1)} async-done(((bf16[2,32,17,2048]{3,0,2,1:T(2,128)(2,1)}), bf16[2,32,17,2048]{3,0,2,1:T(2,128)(2,1)}, u32[]{:S(2)}, u32[]{:S(2)}) %all-to-all-start.2) | async-done | bytes 4456480 | tf_op jit(solution)/shard_map/all_to_all | solution.py:46
  344.6 10.3 %fusion.1 = f32[2,544,768]{2,1,0:T(8,128)} fusion(bf16[2,2048,768]{2,1,0:T(8,128)(2,1)} %param.10, bf16[2,544,2048]{2,0,1:T(2,128)(2,1)} %bitcast.5), kind=kOutput, calls=%fused_computation.14 | convolution fusion | flops 3422552064 | bytes 14090240 | tf_op jit(solution)/shard_map/erd,edf->erf/dot_general | solution.py:51
  354.9 0.0 copy-done
  354.9 0.0 copy-done.1
  354.9 7.6 %multiply_convert_fusion.3 = (bf16[2,544,384]{2,1,0:T(8,128)(2,1)S(1)}, bf16[2,544,384]{2,1,0:T(8,128)(2,1)S(1)}, bf16[2,544,384]{2,1,0:T(8,128)(2,1)S(1)}) fusion(f32[2,544,768]{2,1,0:T(8,128)} %fusion.1, bf16[2,384,2048]{2,1,0:T(8,128)(2,1)S(1)} %copy-done, f32[2,544,2048]{2,0,1:T(2,128)S(1)} %copy-done.1, f32[2,544]{1,0:T(2,128)S(1)} %reshape.208), kind=kOutput, calls=%fused_computation.22 | convolution fusion | flops 1721999360 | bytes 17912064 | tf_op jit(solution)/shard_map/erd,efd->erf/dot_general | solution.py:73
  362.5 0.0 copy-start.4
  362.5 6.4 %fusion.3 = bf16[2048,2,384]{0,2,1:T(8,128)(2,1)S(1)} fusion(bf16[2,544,384]{2,1,0:T(8,128)(2,1)S(1)} %get-tuple-element.19, f32[2,544,2048]{2,0,1:T(2,128)S(1)} %copy-done.1, f32[2,544]{1,0:T(2,128)S(1)} %reshape.208), kind=kOutput, calls=%fused_computation.18 | convolution fusion | flops 1717305344 | bytes 12898560 | tf_op jit(solution)/shard_map/erd,erf->def/dot_general | solution.py:83
  368.9 10.5 %convert_bitcast_fusion = bf16[2048,2,768]{0,2,1:T(8,128)(2,1)S(1)} fusion(bf16[2,544,2048]{2,0,1:T(2,128)(2,1)} %bitcast.5, bf16[2,544,384]{2,1,0:T(8,128)(2,1)S(1)} %get-tuple-element.18, bf16[2,544,384]{2,1,0:T(8,128)(2,1)S(1)} %get-tuple-element.17), kind=kOutput, calls=%fused_computation.9 | convolution fusion | flops 3429040128 | bytes 12419072 | tf_op jit(solution)/shard_map/erd,erf->def/dot_general | solution.py:82
  379.4 8.7 %pad_maximum_fusion = bf16[2048,2,1152]{0,2,1:T(8,128)(2,1)} fusion(bf16[2048,2,384]{0,2,1:T(8,128)(2,1)S(1)} %fusion.3, bf16[2048,2,768]{0,2,1:T(8,128)(2,1)S(1)} %convert_bitcast_fusion), kind=kLoop, calls=%fused_computation.6 | loop fusion | flops 18874368 | bytes 18874368 | tf_op jit(solution)/shard_map/concatenate | solution.py:85
  388.1 0.0 reduce-scatter.2.cloned.1.call-update
  388.2 9.9 %multiply_reduce_fusion = bf16[2,544]{1,0:T(2,128)(2,1)S(1)} fusion(f32[2,544,2048]{2,0,1:T(2,128)} %convert.21, bf16[2,544,384]{2,1,0:T(8,128)(2,1)} %copy-done.2, bf16[2,384,2048]{2,1,0:T(8,128)(2,1)S(1)} %copy-done), kind=kOutput, calls=%fused_computation.7 | convolution fusion | flops 1715731456 | bytes 12896384 | tf_op jit(solution)/shard_map/erf,efd->erd/dot_general | solution.py:58
  398.1 0.1 convert_element_type.58
  398.2 0.6 copy.66
  398.8 8.4 %all-to-all-start.4 = ((bf16[2,32,17]{2,0,1:T(2,128)(2,1)}), bf16[2,32,17]{2,0,1:T(2,128)(2,1)S(1)}, u32[]{:S(2)}, u32[]{:S(2)}) async-start(bf16[2,32,17]{2,0,1:T(2,128)(2,1)} %copy.66), calls=%async_computation.4 | async-start | bytes 32768 | tf_op jit(solution)/shard_map/all_to_all | solution.py:94
  407.2 9.4 %convolution_convert_fusion = bf16[2,544,2048]{2,1,0:T(8,128)(2,1)} fusion(bf16[2,2048,768]{2,1,0:T(8,128)(2,1)} %param.10, bf16[2,544,384]{2,1,0:T(8,128)(2,1)} %copy-done.4, bf16[2,544,384]{2,1,0:T(8,128)(2,1)} %copy-done.3), kind=kOutput, calls=%fused_computation.16 | convolution fusion | flops 3428122624 | bytes 12419072 | tf_op jit(solution)/shard_map/erf,edf->erd/dot_general | solution.py:79
  416.5 9.0 %copy.63 = bf16[2,544,2048]{2,0,1:T(2,128)(2,1)} copy(bf16[2,544,2048]{2,1,0:T(8,128)(2,1)} %convolution_convert_fusion) | data formatting | bytes 8912896 | tf_op jit(solution)/shard_map/convert_element_type | solution.py:81
  425.5 0.0 all-to-all-done.4
  425.6 10.3 %all-to-all-start.3 = ((bf16[2,32,17,2048]{3,0,2,1:T(2,128)(2,1)}), bf16[2,32,17,2048]{3,0,2,1:T(2,128)(2,1)}, u32[]{:S(2)}, u32[]{:S(2)}) async-start(bf16[2,32,17,2048]{3,0,2,1:T(2,128)(2,1)} %bitcast.37), calls=%async_computation.3 | async-start | bytes 8912896 | tf_op jit(solution)/shard_map/all_to_all | solution.py:91
  435.9 0.1 reshape.206
  436.0 6.8 %gather_fusion.4 = bf16[1024]{0:T(1024)(128)(2,1)S(1)} fusion(bf16[1088]{0:T(1024)(128)(2,1)S(1)} %reshape.206, s32[1024]{0:T(1024)S(1)} %broadcast_clamp_fusion), kind=kCustom, calls=%fused_computation.4 | custom fusion | bytes 8192 | tf_op jit(solution)/shard_map/gather | solution.py:106
  442.8 0.1 reshape.207
  442.9 0.7 copy.69
  443.6 94.5 %all-to-all-done.3 = bf16[2,32,17,2048]{3,0,2,1:T(2,128)(2,1)} async-done(((bf16[2,32,17,2048]{3,0,2,1:T(2,128)(2,1)}), bf16[2,32,17,2048]{3,0,2,1:T(2,128)(2,1)}, u32[]{:S(2)}, u32[]{:S(2)}) %all-to-all-start.3) | async-done | bytes 4456480 | tf_op jit(solution)/shard_map/all_to_all | solution.py:91
  538.1 7.4 %copy.64 = bf16[2,32,17,2048]{3,2,1,0:T(8,128)(2,1)} copy(bf16[2,32,17,2048]{3,0,2,1:T(2,128)(2,1)} %all-to-all-done.3) | data formatting | bytes 8912896 | tf_op jit(solution)/shard_map/all_to_all | solution.py:91
  545.5 7.7 %reshape.204 = bf16[1088,2048]{1,0:T(8,128)(2,1)} reshape(bf16[2,32,17,2048]{3,2,1,0:T(8,128)(2,1)} %copy.64) | data formatting | bytes 8912896 | tf_op jit(solution)/shard_map/reshape | solution.py:102
  553.2 11.7 %gather_fusion.3 = bf16[1024,2048]{1,0:T(8,128)(2,1)} fusion(bf16[1088,2048]{1,0:T(8,128)(2,1)} %reshape.204, s32[1024]{0:T(1024)S(1)} %broadcast_clamp_fusion), kind=kCustom, calls=%fused_computation.3 | custom fusion | bytes 8392704 | tf_op jit(solution)/shard_map/gather | solution.py:102
  564.9 5.9 %bitcast_reduce_fusion = bf16[128,2048]{1,0:T(8,128)(2,1)} fusion(bf16[1024,2048]{1,0:T(8,128)(2,1)} %gather_fusion.3), kind=kLoop, calls=%fused_computation.12 | loop fusion | flops 1835008 | bytes 4718592 | tf_op jit(solution)/shard_map/reduce_sum | solution.py:103
  570.8 4.2 copy.70
  (16 shorter events, 0.1 us)
Async XLA Ops:
  7.2 347.7 %copy-start = (bf16[2,384,2048]{2,1,0:T(8,128)(2,1)S(1)}, bf16[2,384,2048]{2,1,0:T(8,128)(2,1)}, u32[]{:S(2)}) copy-start(bf16[2,384,2048]{2,1,0:T(8,128)(2,1)} %param.11) | copy-start | bytes 9437188
  55.5 70.1 %all-to-all-start = ((bf16[2,32,17]{2,0,1:T(2,128)(2,1)}), bf16[2,32,17]{2,0,1:T(2,128)(2,1)S(1)}, u32[]{:S(2)}, u32[]{:S(2)}) async-start(bf16[2,32,17]{2,0,1:T(2,128)(2,1)} %copy.56), calls=%async_computation | async-start | bytes 32768 | tf_op jit(solution)/shard_map/all_to_all | solution.py:48
  125.7 112.6 %all-to-all-start.1 = ((bf16[2,32,17,2048]{3,0,2,1:T(2,128)(2,1)}), bf16[2,32,17,2048]{3,0,2,1:T(2,128)(2,1)}, u32[]{:S(2)}, u32[]{:S(2)}) async-start(bf16[2,32,17,2048]{3,0,2,1:T(2,128)(2,1)} %copy.59), calls=%async_computation.1 | async-start | bytes 8912896 | tf_op jit(solution)/shard_map/all_to_all | solution.py:47
  238.2 106.3 %all-to-all-start.2 = ((bf16[2,32,17,2048]{3,0,2,1:T(2,128)(2,1)}), bf16[2,32,17,2048]{3,0,2,1:T(2,128)(2,1)}, u32[]{:S(2)}, u32[]{:S(2)}) async-start(bf16[2,32,17,2048]{3,0,2,1:T(2,128)(2,1)} %copy.61), calls=%async_computation.2 | async-start | bytes 8912896 | tf_op jit(solution)/shard_map/all_to_all | solution.py:46
  243.4 327.4 %reduce-scatter.2.cloned.1.call-start = ((), (), s32[]{:S(2)}) async-start(), calls=%async_computation.6 | async-start | bytes 10616832 | tf_op jit(solution)/shard_map/reduce_scatter | solution.py:84
  344.6 10.3 %copy-start.1 = (f32[2,544,2048]{2,0,1:T(2,128)S(1)}, f32[2,544,2048]{2,0,1:T(2,128)}, u32[]{:S(2)}) copy-start(f32[2,544,2048]{2,0,1:T(2,128)} %convert.21) | copy-start | bytes 26738692
  362.5 6.4 %copy-start.2 = (bf16[2,544,384]{2,1,0:T(8,128)(2,1)}, bf16[2,544,384]{2,1,0:T(8,128)(2,1)S(1)}, u32[]{:S(2)}) copy-start(bf16[2,544,384]{2,1,0:T(8,128)(2,1)S(1)} %get-tuple-element.19) | copy-start | bytes 2506756
  362.5 6.4 %copy-start.3 = (bf16[2,544,384]{2,1,0:T(8,128)(2,1)}, bf16[2,544,384]{2,1,0:T(8,128)(2,1)S(1)}, u32[]{:S(2)}) copy-start(bf16[2,544,384]{2,1,0:T(8,128)(2,1)S(1)} %get-tuple-element.17) | copy-start | bytes 2506756
  362.5 6.4 %copy-start.4 = (bf16[2,544,384]{2,1,0:T(8,128)(2,1)}, bf16[2,544,384]{2,1,0:T(8,128)(2,1)S(1)}, u32[]{:S(2)}) copy-start(bf16[2,544,384]{2,1,0:T(8,128)(2,1)S(1)} %get-tuple-element.18) | copy-start | bytes 2506756
  398.8 26.7 %all-to-all-start.4 = ((bf16[2,32,17]{2,0,1:T(2,128)(2,1)}), bf16[2,32,17]{2,0,1:T(2,128)(2,1)S(1)}, u32[]{:S(2)}, u32[]{:S(2)}) async-start(bf16[2,32,17]{2,0,1:T(2,128)(2,1)} %copy.66), calls=%async_computation.4 | async-start | bytes 32768 | tf_op jit(solution)/shard_map/all_to_all | solution.py:94
  425.6 112.5 %all-to-all-start.3 = ((bf16[2,32,17,2048]{3,0,2,1:T(2,128)(2,1)}), bf16[2,32,17,2048]{3,0,2,1:T(2,128)(2,1)}, u32[]{:S(2)}, u32[]{:S(2)}) async-start(bf16[2,32,17,2048]{3,0,2,1:T(2,128)(2,1)} %bitcast.37), calls=%async_computation.3 | async-start | bytes 8912896 | tf_op jit(solution)/shard_map/all_to_all | solution.py:91
Sparse Core Ops, SparseCore 0:
  388.3 57.5 reduce-scatter.1
where the time goes:
time: 588 us; the launch traced here: 582 us
  waiting for transfers between devices  277 us (47%)
  local copies, waits for them, and re-layouts  123 us (21%)
  other arithmetic  68 us (12%)
  matrix products  54.1 us (9%)
  starting transfers between devices  45.8 us (8%)
  between operations  14.8 us (3%)
    all_to_all x1, waiting for transfers between devices, on_device(): lax.all_to_all(row_grad.reshape(block_shape), 'expert', split_axis=1, con...  94.5 us
    all_to_all x1, waiting for transfers between devices, on_device(): lax.all_to_all(send_cotangent, 'expert', split_axis=1, concat_axis=1, til...  92.4 us
    all_to_all x1, waiting for transfers between devices, on_device(): lax.all_to_all(send_inputs, 'expert', split_axis=1, concat_axis=1, tiled=...  89.8 us
    another operation x3, other arithmetic  31.3 us
    gather x2, local copies, waits for them, and re-layouts, on_device(): out_grad[owner_token]  19.3 us
    gather x2, local copies, waits for them, and re-layouts, on_device(): tokens[owner_token]  19.3 us
  transfers between devices with their start and end apart: 6, of which 3 were waited for; matrix products, arithmetic and copies ran while one was open for 26% of the time, Pallas kernels for 0%

commit v1 on v0

v1 whole, which is shorter than its diff:
```python
import functools
import jax
import jax.numpy as jnp
from jax import lax
from jax.experimental import pallas as pl
from jax.experimental.pallas import tpu as pltpu
from jax.sharding import PartitionSpec as P

X = 4
CAP = 17
W = 256
H = 128
MESH = pl.DeviceIdType.MESH
F32 = jnp.float32
BF16 = jnp.bfloat16


def dot(a, b, ca=1, cb=0):
    return lax.dot_general(a, b, (((ca,), (cb,)), ((), ())), preferred_element_type=F32)


def ring(v, n):
    return lax.rem(v + n, n)


def at_expert(index):
    return {"expert": index}


def greet(mx, mz, zs):
    barrier = pltpu.get_barrier_semaphore()
    for d in range(1, zs):
        pl.semaphore_signal(
            barrier, inc=1, device_id=at_expert(mx * zs + ring(mz + d, zs)), device_id_type=MESH
        )
    for d in range(1, X):
        pl.semaphore_signal(
            barrier, inc=1, device_id=at_expert(ring(mx + d, X) * zs + mz), device_id_type=MESH
        )
    pl.semaphore_wait(barrier, zs - 1 + X - 1)


def remote(src, dst, send_sem, recv_sem, device):
    return pltpu.make_async_remote_copy(
        src_ref=src,
        dst_ref=dst,
        send_sem=send_sem,
        recv_sem=recv_sem,
        device_id=at_expert(device),
        device_id_type=MESH,
    )


def rows_of(block, n):
    return pl.ds(pl.multiple_of(block * n, n), n)


def dispatch_kernel(
    zs, half, tok, cot, meta, wgu, wd, gp_o, gg_o, mt_o, wp_o,
    zbuf, metab, xmeta, pick, xs, xr, rl, accp, accu, wguv, wdv, hs, wst,
    own_sem, w_sem, wst_sem, z_send, z_recv, x_send, x_recv, r_recv, m_send, m_recv, q_send, q_recv,
):
    t = tok.shape[0]
    ff = wd.shape[1]
    chunks = 2 * half
    rpe = zs * CAP
    rows = 2 * rpe
    expert = lax.axis_index("expert")
    mx, mz = expert // zs, lax.rem(expert, zs)
    zn, zp = mx * zs + ring(mz + 1, zs), mx * zs + ring(mz - 1, zs)
    xn, xp = ring(mx + 1, X) * zs + mz, ring(mx - 1, X) * zs + mz
    far = zs // 2

    w_copies = [
        pltpu.make_async_copy(wgu, wguv, w_sem.at[0]),
        pltpu.make_async_copy(wd, wdv, w_sem.at[1]),
        pltpu.make_async_copy(
            meta.at[mz], metab.at[:, :, rows_of(mz, t)], w_sem.at[2]
        ),
    ]
    own = rows_of(mz, t)

    def own_copy(src, c, lanes):
        return pltpu.make_async_copy(
            src.at[:, pl.ds(pl.multiple_of(lanes * W, W), W)], zbuf.at[c, own], own_sem.at[c]
        )

    @pl.loop(0, half)
    def _(c):
        own_copy(tok, c, c).start()
        own_copy(cot, c + half, c).start()

    for copy in w_copies:
        copy.start()
    greet(mx, mz, zs)

    def meta_copy(d):
        peer = ring(mz + d, zs)
        return remote(
            meta.at[peer], metab.at[:, :, rows_of(mz, t)], m_send.at[d], m_recv.at[d],
            mx * zs + peer,
        )

    for d in range(1, zs):
        meta_copy(d).start()

    def z_copy(c, way, h):
        block = ring(mz - h, zs) if way == 0 else ring(mz + h, zs)
        ref = zbuf.at[c, rows_of(block, t)]
        if h == far - 1:
            ref = zbuf.at[c, rows_of(block, t), pl.ds(way * H, H)]
        return remote(
            ref, ref, z_send.at[c, way, h], z_recv.at[c, way, h], zn if way == 0 else zp
        )

    def z_wait(c, way, h):
        block = ring(mz - h - 1, zs) if way == 0 else ring(mz + h + 1, zs)
        ref = zbuf.at[c, rows_of(block, t)]
        if h == far - 1:
            ref = zbuf.at[c, rows_of(block, t), pl.ds(way * H, H)]
        return remote(
            ref, ref, z_send.at[c, way, h], z_recv.at[c, way, h], zn if way == 0 else zp
        )

    def x_copies(c):
        return (
            remote(xs.at[c, 0], xr.at[c, 1], x_send.at[c, 0], x_recv.at[c, 0], xn),
            remote(xs.at[c, 2], xr.at[c, 3], x_send.at[c, 1], x_recv.at[c, 1], xp),
            remote(
                xs.at[c, 1, :, pl.ds(0, H)], rl.at[c, 0], x_send.at[c, 2], r_recv.at[c, 0], xn
            ),
            remote(
                xs.at[c, 1, :, pl.ds(H, H)], rl.at[c, 1], x_send.at[c, 3], r_recv.at[c, 1], xp
            ),
        )

    def relay_copies(c):
        return (
            remote(
                rl.at[c, 0], xr.at[c, 2, :, pl.ds(0, H)], x_send.at[c, 4], x_recv.at[c, 2], xn
            ),
            remote(
                rl.at[c, 1], xr.at[c, 2, :, pl.ds(H, H)], x_send.at[c, 5], x_recv.at[c, 3], xp
            ),
        )

    def quick_copy(d):
        peer = ring(mx + d, X)
        return remote(
            metab.at[peer], xmeta.at[d], q_send.at[d], q_recv.at[d], peer * zs + mz
        )

    accp[...] = jnp.zeros_like(accp)
    accu[...] = jnp.zeros_like(accu)

    def valid(c):
        return (c >= 0) & (c < chunks)

    @pl.loop(0, chunks + far + 3)
    def _(i):
        @pl.when(i < chunks)
        def _():
            own_copy(tok, i, 0).wait()
            z_copy(i, 0, 0).start()
            z_copy(i, 1, 0).start()

        for h in range(1, far):
            @pl.when(valid(i - h))
            def _():
                c = i - h
                for way in range(2):
                    z_wait(c, way, h - 1).wait_recv()
                    z_copy(c, way, h).start()

        @pl.when(i == far - 1)
        def _():
            w_copies[2].wait()
            for d in range(1, zs):
                meta_copy(d).wait_recv()
            for d in range(1, X):
                quick_copy(d).start()
            for d in range(X):
                peer = ring(mx + d, X)
                first = jnp.broadcast_to(metab[peer, 0:1, :], (16, zs * t))
                second = jnp.broadcast_to(metab[peer, 1:2, :], (16, zs * t))

                @pl.loop(0, rows // 16)
                def _(b):
                    ids = lax.broadcasted_iota(jnp.int32, (16, zs * t), 0) + b * 16
                    slot = ids.astype(F32)
                    hit = jnp.where(ids < rpe, first, second) == slot
                    pick[d, pl.ds(pl.multiple_of(b * 16, 16), 16), :] = jnp.where(
                        hit, 1.0, 0.0
                    ).astype(BF16)

        @pl.when(valid(i - far))
        def _():
            c = i - far
            for way in range(2):
                z_wait(c, way, far - 1).wait_recv()
            for d in (2, 1, 3, 0):
                got = dot(pick[d], zbuf[c]).astype(BF16)
                if d == 0:
                    xr[c, 0] = got
                else:
                    xs[c, d - 1] = got
            direct = x_copies(c)
            for k in (2, 3, 0, 1):
                direct[k].start()

        @pl.when(valid(i - far - 1))
        def _():
            c = i - far - 1
            into = x_copies(c)
            out = relay_copies(c)
            for way in range(2):
                into[2 + way].wait_recv()
                out[way].start()

        @pl.when(i == far + 1)
        def _():
            w_copies[0].wait()
            w_copies[1].wait()

        def arrived(c):
            direct, passed = x_copies(c), relay_copies(c)
            direct[0].wait_recv()
            direct[1].wait_recv()
            passed[0].wait_recv()
            passed[1].wait_recv()

        @pl.when((i >= far + 2) & (i < far + 2 + half))
        def _():
            c = i - far - 2
            arrived(c)

            @pl.loop(0, X)
            def _(s):
                for e in range(2):
                    lo = e * (rpe // 16 * 16)
                    cut = e * rpe - lo
                    part = dot(
                        xr[c, s, pl.ds(lo, rows - rpe // 16 * 16)],
                        wguv[e, pl.ds(pl.multiple_of(c * W, W), W), :],
                    )
                    at = pl.ds(pl.multiple_of(s * rows + e * rpe, 8), rpe)
                    accp[at, :] += part[cut : cut + rpe]

        @pl.when((i >= far + 2 + half) & (i < far + 2 + chunks))
        def _():
            c = i - far - 2
            arrived(c)

            @pl.loop(0, X)
            def _(s):
                for e in range(2):
                    lo = e * (rpe // 16 * 16)
                    cut = e * rpe - lo
                    part = dot(
                        xr[c, s, pl.ds(lo, rows - rpe // 16 * 16)],
                        wdv[e, :, pl.ds(pl.multiple_of((c - half) * W, W), W)],
                        1,
                        1,
                    )
                    at = pl.ds(pl.multiple_of(s * rows + e * rpe, 8), rpe)
                    accu[at, :] += part[cut : cut + rpe]

    for d in range(1, X):
        quick_copy(d).wait_recv()
    xmeta[0] = metab[mx]
    mt_o[...] = metab[...]
    padded = rows - rpe // 16 * 16

    @pl.loop(0, X)
    def _(s):
        sums = []
        for e in range(2):
            at = pl.ds(pl.multiple_of(s * rows + e * rpe, 8), rpe)
            slot = xmeta[s, e : e + 1, :]
            gate_row = xmeta[s, 2 + e : 3 + e, :]
            ids = (lax.broadcasted_iota(jnp.int32, (rpe, zs * t), 0) + e * rpe).astype(F32)
            gate = jnp.sum(jnp.where(slot == ids, gate_row, 0.0), axis=1, keepdims=True)
            gate_pre = accp[at, 0:ff]
            up_pre = accp[at, ff : 2 * ff]
            logistic = jax.nn.sigmoid(gate_pre)
            active = gate_pre * logistic
            slope = logistic * (1.0 + gate_pre * (1.0 - logistic))
            hidden = (active * up_pre).astype(BF16).astype(F32)
            u = accu[at, :]
            sums.append(jnp.sum(hidden * u, axis=1, keepdims=True))
            gh = gate * u
            full = jnp.concatenate([gh * up_pre * slope, gh * active], axis=1)
            scaled_hidden = gate * hidden
            gap = padded - rpe
            if e == 0:
                full = jnp.concatenate([full, jnp.zeros((gap, 2 * ff), F32)], axis=0)
                scaled_hidden = jnp.concatenate([scaled_hidden, jnp.zeros((gap, ff), F32)], axis=0)
            else:
                full = jnp.concatenate([jnp.zeros((gap, 2 * ff), F32), full], axis=0)
                scaled_hidden = jnp.concatenate([jnp.zeros((gap, ff), F32), scaled_hidden], axis=0)
            gp_o[e, s] = full.astype(BF16)
            hs[e, s] = scaled_hidden.astype(BF16)
        wide = gg_o.shape[2]
        column = jnp.concatenate(sums + [jnp.zeros((wide - rows, 1), F32)], axis=0)
        a = lax.broadcasted_iota(jnp.int32, (wide, wide), 0)
        b = lax.broadcasted_iota(jnp.int32, (wide, wide), 1)
        diagonal = jnp.where(a == b, column, 0.0).astype(BF16)
        row = lax.broadcasted_iota(jnp.int32, (16, wide), 0)
        lane = lax.broadcasted_iota(jnp.int32, (16, wide), 1)
        mine = ((row == 0) & (lane < rpe)) | ((row == 1) & (lane >= rpe) & (lane < rows))
        gg_o[s] = dot(jnp.where(mine, 1.0, 0.0).astype(BF16), diagonal).astype(BF16)

    def out_copy(c, slot):
        return pltpu.make_async_copy(wst.at[slot], wp_o.at[c], wst_sem.at[slot])

    @pl.loop(0, half)
    def _(c):
        slot = lax.rem(c, 2)

        @pl.when(c >= 2)
        def _():
            out_copy(c, slot).wait()

        for e in range(2):
            lo = e * (rpe // 16 * 16)
            first = dot(xr[c, 0, pl.ds(lo, padded)], gp_o[e, 0], 0, 0)
            second = dot(xr[c + half, 0, pl.ds(lo, padded)], hs[e, 0], 0, 0)
            for s in range(1, X):
                first += dot(xr[c, s, pl.ds(lo, padded)], gp_o[e, s], 0, 0)
                second += dot(xr[c + half, s, pl.ds(lo, padded)], hs[e, s], 0, 0)
            wst[slot, e, :, 0 : 2 * ff] = first.astype(BF16)
            wst[slot, e, :, 2 * ff : 3 * ff] = second.astype(BF16)
        out_copy(c, slot).start()

    for c in range(half - 2, half):
        out_copy(c, c % 2).wait()
    for d in range(1, zs):
        meta_copy(d).wait_send()
    for d in range(1, X):
        quick_copy(d).wait_send()

    @pl.loop(0, chunks)
    def _(c):
        for h in range(far):
            for way in range(2):
                z_copy(c, way, h).wait_send()
        for copy in x_copies(c) + relay_copies(c):
            copy.wait_send()


def combine_kernel(
    zs, half, gp, gg, mt, wgu, out, dp_o,
    wguv, pick, rs, rr, rl, part, zo, zi, ggr, dps, dpr,
    w_sem, z_send, z_recv, x_send, x_recv, r_recv, g_send, g_recv, d_send, d_recv,
):
    t = out.shape[0]
    rpe = zs * CAP
    rows = 2 * rpe
    wide = gg.shape[2]
    padded = rows - rpe // 16 * 16
    expert = lax.axis_index("expert")
    mx, mz = expert // zs, lax.rem(expert, zs)
    zn, zp = mx * zs + ring(mz + 1, zs), mx * zs + ring(mz - 1, zs)
    xn, xp = ring(mx + 1, X) * zs + mz, ring(mx - 1, X) * zs + mz
    far = zs // 2

    w_copy = pltpu.make_async_copy(wgu, wguv, w_sem.at[0])
    w_copy.start()
    greet(mx, mz, zs)

    def gate_copy(s):
        return remote(
            gg.at[s], ggr.at[s], g_send.at[s], g_recv.at[s], ring(mx - s, X) * zs + mz
        )

    for s in range(1, X):
        gate_copy(s).start()

    for d in range(X):
        peer = ring(mx + d, X)
        first = jnp.broadcast_to(mt[peer, 0:1, :], (16, zs * t))
        second = jnp.broadcast_to(mt[peer, 1:2, :], (16, zs * t))

        @pl.loop(0, wide // 16)
        def _(b):
            ids = lax.broadcasted_iota(jnp.int32, (16, zs * t), 0) + b * 16
            slot = ids.astype(F32)
            hit = jnp.where(ids < rpe, first, second) == slot
            pick[d, pl.ds(pl.multiple_of(b * 16, 16), 16), :] = jnp.where(hit, 1.0, 0.0).astype(
                BF16
            )

    w_copy.wait()

    def x_copies(c):
        return (
            remote(rs.at[c, 0], rr.at[c, 1], x_send.at[c, 0], x_recv.at[c, 0], xp),
            remote(rs.at[c, 2], rr.at[c, 3], x_send.at[c, 1], x_recv.at[c, 1], xn),
            remote(
                rs.at[c, 1, :, pl.ds(0, H)], rl.at[c, 0], x_send.at[c, 2], r_recv.at[c, 0], xp
            ),
            remote(
                rs.at[c, 1, :, pl.ds(H, H)], rl.at[c, 1], x_send.at[c, 3], r_recv.at[c, 1], xn
            ),
        )

    def relay_copies(c):
        return (
            remote(
                rl.at[c, 0], rr.at[c, 2, :, pl.ds(0, H)], x_send.at[c, 4], x_recv.at[c, 2], xp
            ),
            remote(
                rl.at[c, 1], rr.at[c, 2, :, pl.ds(H, H)], x_send.at[c, 5], x_recv.at[c, 3], xn
            ),
        )

    def z_copy(c, way, h):
        src, dst = zo.at[c, way, h], zi.at[c, way, h]
        if h == 0:
            src, dst = src.at[:, pl.ds(way * H, H)], dst.at[:, pl.ds(way * H, H)]
        return remote(
            src, dst, z_send.at[c, way, h], z_recv.at[c, way, h], zn if way == 0 else zp
        )

    def piece(c, block):
        return part[c, rows_of(block, t), :]

    def valid(c):
        return (c >= 0) & (c < half)

    def probs_copy(d):
        peer = ring(mz + d, zs)
        return remote(
            dps.at[:, :, rows_of(peer, t)], dpr.at[mz], d_send.at[d], d_recv.at[d],
            mx * zs + peer,
        )

    def probs_wait(d):
        peer = ring(mz - d, zs)
        return remote(
            dps.at[:, :, rows_of(peer, t)], dpr.at[peer], d_send.at[d], d_recv.at[d],
            mx * zs + peer,
        )

    @pl.loop(0, half + far + 2)
    def _(i):
        @pl.when(i < half)
        def _():
            lanes = rows_of(i, W)
            for s in (2, 1, 3, 0):
                both = []
                for e in range(2):
                    res = dot(gp[e, s], wguv[e, lanes, :], 1, 1)
                    cut = e * (padded - rpe)
                    both.append(res[cut : cut + rpe])
                got = jnp.concatenate(both, axis=0).astype(BF16)
                if s == 0:
                    rr[i, 0] = got
                else:
                    rs[i, s - 1] = got
            direct = x_copies(i)
            for k in (2, 3, 0, 1):
                direct[k].start()

        @pl.when(i == 1)
        def _():
            for s in range(1, X):
                gate_copy(s).wait_recv()
            ggr[0] = gg[0]
            for d in range(X):
                dps[d] = dot(ggr[d], pick[d])
            for d in range(1, zs):
                probs_copy(d).start()

        @pl.when(valid(i - 1))
        def _():
            c = i - 1
            into, onward = x_copies(c), relay_copies(c)
            for way in range(2):
                into[2 + way].wait_recv()
                onward[way].start()

        @pl.when(valid(i - 2))
        def _():
            c = i - 2
            direct, passed = x_copies(c), relay_copies(c)
            direct[0].wait_recv()
            direct[1].wait_recv()
            passed[0].wait_recv()
            passed[1].wait_recv()
            total = dot(pick[0, 0:rows, :], rr[c, 0], 0, 0)
            for d in range(1, X):
                total += dot(pick[d, 0:rows, :], rr[c, d], 0, 0)
            part[c] = total
            for way in range(2):
                zo[c, way, 0] = piece(c, ring(mz + far, zs)).astype(BF16)
                z_copy(c, way, 0).start()

        for h in range(1, far):
            @pl.when(valid(i - 2 - h))
            def _():
                c = i - 2 - h
                for way in range(2):
                    z_copy(c, way, h - 1).wait_recv()
                    block = ring(mz + far - h, zs) if way == 0 else ring(mz - far + h, zs)
                    mine = piece(c, block)
                    if h == 1:
                        side = pl.ds(way * H, H)
                        other = pl.ds(H - way * H, H)
                        lo, hi = way * H, H - way * H
                        zo[c, way, h, :, side] = (
                            mine[:, lo : lo + H] + zi[c, way, 0, :, side].astype(F32)
                        ).astype(BF16)
                        zo[c, way, h, :, other] = mine[:, hi : hi + H].astype(BF16)
                    else:
                        zo[c, way, h] = (mine + zi[c, way, h - 1].astype(F32)).astype(BF16)
                    z_copy(c, way, h).start()

        @pl.when(valid(i - 2 - far))
        def _():
            c = i - 2 - far
            for way in range(2):
                z_copy(c, way, far - 1).wait_recv()
            total = piece(c, mz)
            total += zi[c, 0, far - 1].astype(F32) + zi[c, 1, far - 1].astype(F32)
            out[:, rows_of(c, W)] = total.astype(BF16)

    dpr[mz] = dps[:, :, rows_of(mz, t)]
    for d in range(1, zs):
        probs_wait(d).wait_recv()
    dp_o[...] = dpr[...]
    for d in range(1, zs):
        probs_copy(d).wait_send()
    for s in range(1, X):
        gate_copy(s).wait_send()

    @pl.loop(0, half)
    def _(c):
        for h in range(far):
            for way in range(2):
                z_copy(c, way, h).wait_send()
        for copy in x_copies(c) + relay_copies(c):
            copy.wait_send()


def on_device(tokens, out_grad, expert_ids, gate_probs, gate_up_weight, down_weight):
    t, width = tokens.shape
    top = expert_ids.shape[1]
    ff = down_weight.shape[1]
    zs = lax.axis_size("expert") // X
    experts = 2 * X * zs
    half = width // W
    chunks = 2 * half
    far = zs // 2
    rpe = zs * CAP
    rows = 2 * rpe
    padded = rows - rpe // 16 * 16
    wide = -(-rows // 128) * 128
    mz = lax.rem(lax.axis_index("expert"), zs)

    named = expert_ids.T[:, None, :] == jnp.arange(experts, dtype=jnp.int32)[None, :, None]
    hit = jnp.any(named, axis=0)
    gates = jnp.sum(jnp.where(named, gate_probs.T[:, None, :].astype(F32), 0.0), axis=0)
    before = (
        jnp.arange(t, dtype=jnp.int32)[:, None] < jnp.arange(t, dtype=jnp.int32)[None, :]
    )
    rank = jnp.dot(hit.astype(BF16), before.astype(BF16), preferred_element_type=F32)
    base = mz * CAP + (jnp.arange(experts, dtype=jnp.int32) % 2) * rpe
    slots = jnp.where(hit, rank + base.astype(F32)[:, None], -1.0)
    both = jnp.stack([slots, gates]).reshape(2, X, zs, 2, t)
    meta = jnp.pad(
        both.transpose(2, 1, 0, 3, 4).reshape(zs, X, 4, t), ((0, 0), (0, 0), (0, 4), (0, 0))
    )

    hbm = pl.BlockSpec(memory_space=pltpu.MemorySpace.HBM)
    vmem = pl.BlockSpec(memory_space=pltpu.MemorySpace.VMEM)
    dma = pltpu.SemaphoreType.DMA
    gp, gg, mt, weight_part = pl.pallas_call(
        functools.partial(dispatch_kernel, zs, half),
        out_shape=(
            jax.ShapeDtypeStruct((2, X, padded, 2 * ff), BF16),
            jax.ShapeDtypeStruct((X, 16, wide), BF16),
            jax.ShapeDtypeStruct((X, 8, zs * t), F32),
            jax.ShapeDtypeStruct((half, 2, W, 3 * ff), BF16),
        ),
        in_specs=[hbm] * 5,
        out_specs=(vmem, vmem, vmem, hbm),
        scratch_shapes=[
            pltpu.VMEM((chunks, zs * t, W), BF16),
            pltpu.VMEM((X, 8, zs * t), F32),
            pltpu.VMEM((X, 8, zs * t), F32),
            pltpu.VMEM((X, rows, zs * t), BF16),
            pltpu.VMEM((chunks, X - 1, rows, W), BF16),
            pltpu.VMEM((chunks, X, rows, W), BF16),
            pltpu.VMEM((chunks, 2, rows, H), BF16),
            pltpu.VMEM((X * rows, 2 * ff), F32),
            pltpu.VMEM((X * rows, ff), F32),
            pltpu.VMEM((2, width, 2 * ff), BF16),
            pltpu.VMEM((2, ff, width), BF16),
            pltpu.VMEM((2, X, padded, ff), BF16),
            pltpu.VMEM((2, 2, W, 3 * ff), BF16),
            dma((chunks,)),
            dma((3,)),
            dma((2,)),
            dma((chunks, 2, far)),
            dma((chunks, 2, far)),
            dma((chunks, 6)),
            dma((chunks, 4)),
            dma((chunks, 2)),
            dma((zs,)),
            dma((zs,)),
            dma((X,)),
            dma((X,)),
        ],
        compiler_params=pltpu.CompilerParams(
            collective_id=0, has_side_effects=True, vmem_limit_bytes=61 * 1024 * 1024
        ),
        cost_estimate=pl.CostEstimate(
            flops=20_000_000_000, bytes_accessed=30_000_000, transcendentals=0
        ),
        name="dispatch",
    )(tokens, out_grad, meta, gate_up_weight, down_weight)

    summed = lax.psum_scatter(weight_part, "dp", scatter_dimension=0, tiled=True)

    grad_tokens, probs = pl.pallas_call(
        functools.partial(combine_kernel, zs, half),
        out_shape=(
            jax.ShapeDtypeStruct((t, width), BF16),
            jax.ShapeDtypeStruct((zs, X, 16, t), F32),
        ),
        in_specs=[vmem, vmem, vmem, hbm],
        out_specs=(vmem, vmem),
        scratch_shapes=[
            pltpu.VMEM((2, width, 2 * ff), BF16),
            pltpu.VMEM((X, wide, zs * t), BF16),
            pltpu.VMEM((half, X - 1, rows, W), BF16),
            pltpu.VMEM((half, X, rows, W), BF16),
            pltpu.VMEM((half, 2, rows, H), BF16),
            pltpu.VMEM((half, zs * t, W), F32),
            pltpu.VMEM((half, 2, far, t, W), BF16),
            pltpu.VMEM((half, 2, far, t, W), BF16),
            pltpu.VMEM((X, 16, wide), BF16),
            pltpu.VMEM((X, 16, zs * t), F32),
            pltpu.VMEM((zs, X, 16, t), F32),
            dma((1,)),
            dma((half, 2, far)),
            dma((half, 2, far)),
            dma((half, 6)),
            dma((half, 4)),
            dma((half, 2)),
            dma((X,)),
            dma((X,)),
            dma((zs,)),
            dma((zs,)),
        ],
        compiler_params=pltpu.CompilerParams(
            collective_id=1, has_side_effects=True, vmem_limit_bytes=61 * 1024 * 1024
        ),
        cost_estimate=pl.CostEstimate(
            flops=60_000_000_000, bytes_accessed=100_000_000, transcendentals=0
        ),
        name="combine",
    )(gp, gg, mt, gate_up_weight)

    mx = lax.axis_index("expert") // zs
    order = (jnp.arange(X, dtype=jnp.int32) - mx) % X
    by_expert = probs[:, :, 0:2, :][:, order]
    by_expert = by_expert.transpose(1, 0, 2, 3).reshape(experts, t)
    grad_probs = jnp.sum(jnp.where(named, by_expert[None], 0.0), axis=1).T.astype(BF16)
    grad_weights = summed.transpose(0, 2, 1, 3).reshape(-1, 2, 3 * ff)
    return (grad_tokens, grad_probs, grad_weights)


def solution(mesh):
    split = P(("dp", "expert"), None)
    return jax.shard_map(
        on_device,
        mesh=mesh,
        in_specs=(split, split, split, split, P("expert", None, None), P("expert", None, None)),
        out_specs=(split, split, P("dp", "expert", None)),
        check_vma=False,
    )
```

time: 588 us -> 255 us (0.43)
  waiting for transfers between devices: 277 us -> 0.02 us
  Pallas kernels: 0 us -> 229 us
  local copies, waits for them, and re-layouts: 123 us -> 7.59 us
  other arithmetic: 68 us -> 2.86 us
  matrix products: 54.1 us -> 0.09 us
  starting transfers between devices: 45.8 us -> 0.04 us
    all_to_all x5 -> x0, waiting for transfers between devices: 277 us -> none  [the longest x1 94.5 us: on_device(): lax.all_to_all(row_grad.reshape(block_shape), 'expert', split_axis=1, con...]
    pallas_call x0 -> x2, Pallas kernels: none -> 229 us  [the longest x1 150 us: on_device(): pl.pallas_call(functools.partial(dispatch_kernel, zs, half), out_shape=(j...]
    gather x7 -> x1, local copies, waits for them, and re-layouts: 64 us -> 0.6 us  [on_device(): by_expert = probs[:, :, 0:2, :][:, order]]
    dot_general x6 -> x1, matrix products: 54.1 us -> 0.09 us  [on_device(): jnp.dot(hit.astype(BF16), before.astype(BF16), preferred_element_type=F32)]
    all_to_all x5 -> x0, starting transfers between devices: 45.7 us -> none  [the longest x1 11.5 us: on_device(): lax.all_to_all(send_weights, 'expert', split_axis=1, concat_axis=1, tiled...]
    another operation x3 -> x0, other arithmetic: 31.3 us -> none
    select_n x2 -> x0, local copies, waits for them, and re-layouts: 19.3 us -> none  [the longest x1 9.7 us: on_device(): jnp.where(filled[:, None], tokens[owner_token], 0).reshape(block_shape)]
    convert_element_type x2, other arithmetic: 11.7 us -> 0.69 us  [the longest x1 0.69 us: on_device(): gate_probs.T[:, None, :].astype(F32)]
  transfers between devices with their start and end apart: 6 -> 1, of which waited for: 3 -> 0; matrix products, arithmetic and copies ran while one was open for 26% -> 1% of each run, Pallas kernels for 0% -> 31%
where the time goes in v1:
time: 255 us; the launch traced here: 253 us
  Pallas kernels  229 us (90%)
  between operations  14.1 us (6%)
  local copies, waits for them, and re-layouts  7.59 us (3%)
  other arithmetic  2.86 us (1%)
    pallas_call x1, Pallas kernels, on_device(): pl.pallas_call(functools.partial(dispatch_kernel, zs, half), out_shape=(j...  150 us
    pallas_call x1, Pallas kernels, on_device(): pl.pallas_call(functools.partial(combine_kernel, zs, half), out_shape=(ja...  78.6 us
    unnamed x4, local copies, waits for them, and re-layouts  5.38 us
  transfers between devices with their start and end apart: 1, of which 0 were waited for; matrix products, arithmetic and copies ran while one was open for 1% of the time, Pallas kernels for 31%

profile of v1, /device:TPU:24, one launch (start us, length us, event | category | flops | bytes accessed | tf_op | source)
XLA Modules:
  0.0 253.4 jit_solution(8258325320865837959)
XLA Ops:
  7.2 0.0 reduce-scatter.2.cloned.1.call-start
  7.2 0.7 fusion.1
  8.0 0.7 convert_bitcast_fusion
  8.6 0.7 select_reduce_fusion.1
  9.4 0.1 fusion
  9.5 0.1 maximum_bitcast_fusion
  9.6 0.7 pad.4.meta
  10.2 150.1 %dispatch.1 = (bf16[2,4,144,768]{3,2,1,0:T(8,128)(2,1)}, bf16[4,16,384]{2,1,0:T(8,128)(2,1)}, f32[4,8,1024]{2,1,0:T(8,128)}, bf16[8,2,256,1152]{3,2,1,0:T(8,128)(2,1)}) custom-call(bf16[128,2048]{1,0:T(8,128)(2,1)} %tok.1, bf16[128,2048]{1,0:T(8,128)(2,1)} %cot.1, f32[8,4,8,128]{3,2,1,0:T(8,128)} %pad.4.meta, bf16[2,2048,768]{2,1,0:T(8,128)(2,1)} %wgu.3, ...), custom_call_target="tpu_custom_call" | custom-call | flops 20000000000 | bytes 30000000 | tf_op jit(solution)/shard_map/dispatch/pallas_call | solution.py:578
  160.4 0.0 reduce-scatter.2.cloned.1.call-update
  160.4 0.0 copy-start
  160.4 78.6 %combine.1 = (bf16[128,2048]{1,0:T(8,128)(2,1)}, f32[8,4,16,128]{3,2,1,0:T(8,128)}) custom-call(bf16[2,4,144,768]{3,2,1,0:T(8,128)(2,1)} %get-tuple-element.9.gp, bf16[4,16,384]{2,1,0:T(8,128)(2,1)} %get-tuple-element.10.gg, f32[4,8,1024]{2,1,0:T(8,128)} %get-tuple-element.11.mt, bf16[2,2048,768]{2,1,0:T(8,128)(2,1)} %wgu.3), custom_call_target="tpu_custom_call" | custom-call | flops 60000002048 | bytes 100000000 | tf_op jit(solution)/shard_map/combine/pallas_call | solution.py:626
  239.0 0.9 slice.3
  240.0 0.6 gather_fusion
  240.6 0.0 copy-done
  240.6 0.6 select_reduce_fusion
  241.2 0.0 reduce-scatter.2.cloned.1.call-done
  241.2 3.5 %copy.14 = bf16[256,2,1152]{2,1,0:T(2,128)(2,1)} copy(bf16[256,2,1152]{2,0,1:T(8,128)(2,1)} %bitcast.18) | data formatting | bytes 2359296
  244.7 1.9 copy.16
  (4 shorter events, 0.1 us)
Async XLA Ops:
  7.2 234.1 %reduce-scatter.2.cloned.1.call-start = ((), (), s32[]{:S(2)}) async-start(), calls=%async_computation.1 | async-start | bytes 10616832 | tf_op jit(solution)/shard_map/reduce_scatter | solution.py:624
  160.4 80.2 %copy-start = (s32[128,8]{0,1:T(8,128)S(1)}, s32[128,8]{0,1:T(8,128)}, u32[]{:S(2)}) copy-start(s32[128,8]{0,1:T(8,128)} %param.8) | copy-start | bytes 12292
Sparse Core Ops, SparseCore 0:
  160.5 55.0 reduce-scatter.1
